TPU v7x, 32 devices: a whole 2x2x4 slice. The times are simulated.
32 devices in a mesh: row: 8 (over z, y), col: 4 (over x, core).
Axes of the slice: x: 2, y: 2, z: 4, core: 2. Of those that a mesh axis runs over, the one named last changes fastest.
Arguments:
- x_blocks: bfloat16 [128, 8, 128, 128], P('row', 'col')
- x_cols: int32 [128, 8], P('row', 'col'), may hold values from 0 to 31, as said below
- x_count: int32 [128, 4], P('row', 'col'), may hold values from 0 to 2, as said below
- y_cols: int32 [128, 48], P('row', 'col'), may hold values from 0 to 31, as said below
- y_count: int32 [128, 4], P('row', 'col'), may hold values from 0 to 12, as said below
- branch_flag: int32 [128], P('row'), may hold values from 0 to 1
Outputs:
- new_blocks: bfloat16 [128, 48, 128, 128], P('row', 'col')
- new_trace: float32 [1], replicated
Inputs may be any that keep to these rules, and one draw needn't show every extreme that they name: `x_cols`: within one block row and one column group, the first x_count slots name distinct block columns; other slots hold arbitrary valid columns. Slot 0 of block row I in group I // 32 names column I % 32. `x_count`: reaches 2; at least 1 for block row I in group I // 32. `y_cols`: within one block row and one column group, the first y_count slots name distinct block columns. Slot 0 of block row I in group I // 32 names column I % 32. `y_count`: reaches 12; at least 1 for block row I in group I // 32.
All inputs are finite; a program needn't handle non-finite values.
Results may differ from a plain program's by a relative error of at most 0.0004.
Values may be sent and summed in bfloat16 or wider, within the bound.
No kernel may reach another device: no remote copies, remote signals or barrier semaphores. Data moves between devices by JAX's collectives and lax.ppermute only.
A program may use at most 128 MiB of HBM per device.

v0:
```python
import jax
import jax.numpy as jnp
from jax import lax
from jax.sharding import PartitionSpec as P

NB = 128
ROWCAP = 2


def pick_blocks(blocks, cols, count, block_keys, wanted, active, offset):
    height = cols.shape[0]
    slot_count = cols.shape[1]
    relative = block_keys - offset
    inside = (relative >= 0) & (relative < height) & active
    clipped = jnp.clip(relative, 0, height - 1).astype(jnp.int32)
    slot_ids = jnp.arange(slot_count, dtype=jnp.int32)
    matched = (
        (cols[clipped] == wanted[..., None])
        & (slot_ids < count[clipped, 0][..., None])
        & inside[..., None]
    )
    found = jnp.any(matched, axis=-1)
    picked = jnp.sum(jnp.where(matched, slot_ids, 0), axis=-1)
    flat_blocks = blocks.reshape((height * slot_count,) + blocks.shape[2:])
    chosen = flat_blocks[clipped * slot_count + picked]
    return jnp.where(found[..., None, None], chosen, jnp.zeros((), blocks.dtype))


def pair_keys(row_cols, row_count, y_cols, y_count, col_width, slot_count):
    pairs = row_cols.shape[1]
    ycap = y_cols.shape[1]
    pair_ids = jnp.arange(pairs, dtype=jnp.int32)
    groups = pair_ids // slot_count
    block_keys = groups[None, :] * col_width + row_cols
    live = (pair_ids % slot_count)[None, :] < jnp.take(row_count, groups, axis=1)
    y_live = jnp.arange(ycap, dtype=jnp.int32)[None, :] < y_count
    shape = (row_cols.shape[0], ycap, pairs)
    block_keys = jnp.broadcast_to(block_keys[:, None, :], shape)
    wanted = jnp.broadcast_to(y_cols[:, :, None], shape)
    active = live[:, None, :] & y_live[:, :, None]
    return (block_keys, wanted, active)


def contract(row_blocks, panel, block_keys, wanted, active, offset):

    def one_row(items):
        row_block, keys, targets, flags = items
        chosen = pick_blocks(panel[0], panel[1], panel[2], keys, targets, flags, offset)
        return jnp.einsum("pab,ypbc->yac", row_block, chosen, preferred_element_type=jnp.float32)

    return lax.map(one_row, (row_blocks, block_keys, wanted, active))


def finish(
    product, own_blocks, own_cols, own_count, y_cols, y_count, branch_flag, row_start, col_start
):
    ycap = y_cols.shape[1]
    y_live = jnp.arange(ycap, dtype=jnp.int32)[None, :] < y_count
    slot_ids = jnp.arange(own_cols.shape[1], dtype=jnp.int32)
    own_match = (own_cols[:, None, :] == y_cols[:, :, None]) & (
        slot_ids[None, None, :] < own_count[:, :, None]
    )
    own_term = jnp.einsum(
        "iyq,iqab->iyab", own_match.astype(jnp.float32), own_blocks.astype(jnp.float32)
    )
    flip = (branch_flag == 1)[:, None, None, None]
    updated = jnp.where(flip, 2.0 * own_term - product, product)
    updated = jnp.where(y_live[..., None, None], updated, jnp.zeros((), updated.dtype))
    rows_global = row_start + jnp.arange(y_cols.shape[0], dtype=jnp.int32)[:, None]
    cols_global = col_start + y_cols
    diagonal = (rows_global == cols_global) & y_live
    traces = jnp.trace(updated, axis1=2, axis2=3)
    trace_part = jnp.sum(jnp.where(diagonal, traces, jnp.zeros((), traces.dtype)))
    return (updated.astype(jnp.bfloat16), trace_part)


def on_device(x_blocks, x_cols, x_count, y_cols, y_count, branch_flag):
    row_blocks, row_cols, row_count = (
        lax.all_gather(x_blocks, "col", axis=1, tiled=True),
        lax.all_gather(x_cols, "col", axis=1, tiled=True),
        lax.all_gather(x_count, "col", axis=1, tiled=True),
    )
    col_width = NB // lax.axis_size("col")
    block_keys, wanted, active = pair_keys(row_cols, row_count, y_cols, y_count, col_width, ROWCAP)
    panel = (
        lax.all_gather(x_blocks, "row", axis=0, tiled=True),
        lax.all_gather(x_cols, "row", axis=0, tiled=True),
        lax.all_gather(x_count, "row", axis=0, tiled=True),
    )
    product = contract(row_blocks, panel, block_keys, wanted, active, 0)
    row_start = lax.axis_index("row") * x_blocks.shape[0]
    col_start = lax.axis_index("col") * col_width
    updated, trace_part = finish(
        product, x_blocks, x_cols, x_count, y_cols, y_count, branch_flag, row_start, col_start
    )
    total = lax.psum(trace_part, ("row", "col"))
    return (updated, total.reshape((1,)))


def solution(mesh):
    return jax.shard_map(
        on_device,
        mesh=mesh,
        in_specs=(
            P("row", "col", None, None),
            P("row", "col"),
            P("row", "col"),
            P("row", "col"),
            P("row", "col"),
            P("row"),
        ),
        out_specs=(P("row", "col", None, None), P()),
        check_vma=False,
    )
```

profile of v0, /device:TPU:0, one launch (start us, length us, event | category | flops | bytes accessed | tf_op | source)
XLA Modules:
  0.0 493.7 jit_solution(7032172679561146887)
XLA Ops:
  8.7 6.2 %all-gather.2 = s32[4,1,16]{2,1,0:T(1,128)S(1)} all-gather(s32[1,1,16]{2,1,0:T(1,128)} %bitcast.93), channel_id=1, replica_groups=mesh['row'=8,'col'=4] {'col'}, dimensions={0}, use_global_device_ids=true | all-gather | bytes 320 | tf_op jit(solution)/shard_map/all_gather | solution.py:81
  16.4 5.5 %all-gather = s32[4,2,16]{2,1,0:T(2,128)S(1)} all-gather(s32[1,2,16]{2,1,0:T(2,128)} %bitcast.91), channel_id=1, replica_groups=mesh['row'=8,'col'=4] {'col'}, dimensions={0}, use_global_device_ids=true | all-gather | bytes 640 | tf_op jit(solution)/shard_map/all_gather | solution.py:80
  22.1 21.3 %all-gather.1 = s32[8,16,2]{1,2,0:T(2,128)S(1)} all-gather(s32[1,16,2]{1,2,0:T(2,128)} %bitcast.92), channel_id=1, replica_groups=mesh['row'=8,'col'=4] {'row'}, dimensions={0}, use_global_device_ids=true | all-gather | bytes 1152 | tf_op jit(solution)/shard_map/all_gather | solution.py:87
  46.1 6.8 %all-reduce.1 = s32[128]{0:T(128)S(1)} all-reduce(s32[128]{0:T(128)S(1)} %bitcast_dynamic-update-slice_fusion), channel_id=1, replica_groups=mesh['row'=8,'col'=4] {'row'}, use_global_device_ids=true, to_apply=%add.1 | all-reduce | flops 128 | bytes 1024
  55.2 118.2 %all-gather.6.cloned.1.call-done = bf16[128,2,128,128]{3,2,1,0:T(8,128)(2,1)} async-done(((bf16[16,2,128,128]{3,2,1,0:T(8,128)(2,1)}), bf16[128,2,128,128]{3,2,1,0:T(8,128)(2,1)}) %all-gather.6.cloned.1.call-update) | async-done | bytes 8388624 | tf_op jit(solution)/shard_map/all_gather | solution.py:86
  174.2 233.5 %while.10 = (s32[]{:T(128)}, f32[16,12,128,128]{2,3,1,0:T(8,128)}, s32[16,12,8]{1,2,0:T(8,128)S(1)}, s32[128,2]{1,0:T(8,128)S(1)}, s32[16,12,8]{1,2,0:T(8,128)S(...) while((s32[]{:T(128)}, f32[16,12,128,128]{2,3,1,0:T(8,128)}, ...), condition=%wide.region_3.4_spmd, body=%wide.region_0.3_spmd.sunk | while | flops 404230784 | bytes 16804500 | solution.py:51
  177.6 4.5 gather_fusion.2
  192.2 4.5 gather_fusion.2
  206.8 4.5 gather_fusion.2
  221.4 4.5 gather_fusion.2
  235.9 4.5 gather_fusion.2
  250.5 4.5 gather_fusion.2
  265.1 4.5 gather_fusion.2
  279.7 4.5 gather_fusion.2
  294.3 4.5 gather_fusion.2
  308.9 4.5 gather_fusion.2
  323.4 4.5 gather_fusion.2
  338.1 4.5 gather_fusion.2
  352.7 4.5 gather_fusion.2
  367.3 4.5 gather_fusion.2
  407.6 17.6 %copy.52 = f32[16,12,128,128]{3,1,2,0:T(8,128)} copy(f32[16,12,128,128]{2,3,1,0:T(8,128)} %get-tuple-element.49) | data formatting | bytes 25165824 | tf_op jit(solution)/shard_map/while | solution.py:51
  425.3 14.4 %select_reduce_fusion.1 = (f32[16,12]{1,0:T(8,128)S(1)}, bf16[16,12,128,128]{3,1,2,0:T(8,128)(2,1)}) fusion(pred[128,128]{1,0:T(8,128)(4,1)S(1)} %iota_compare_fusion.1, f32[16,12,128,128]{3,1,2,0:T(8,128)} %copy.52, bf16[16,2,128,128]{3,2,1,0:T(8,128)(2,1)S(1)} %copy-done, pred[16,2]{1,0:T(8,128)(4,1)S(1)} %iota_compare_fusion.2, ...), kind=kOutput, calls=%fused_computation.30 | convolution fusion | flops 34603584 | bytes 19941232 | tf_op jit(solution)/shard_map/iyq,iqab->iyab/dot_general | solution.py:63
  440.4 38.5 %psum.7 = f32[1]{0:T(128)} all-reduce(f32[1]{0:T(128)} %bitcast.30), channel_id=1, replica_groups=mesh['row'=8,'col'=4] {'row','col'}, use_global_device_ids=true, to_apply=%region_6.7 | all-reduce | flops 1 | bytes 8 | tf_op jit(solution)/shard_map/psum | solution.py:96
  478.9 8.0 %copy.54 = bf16[16,12,128,128]{3,2,1,0:T(8,128)(2,1)} copy(bf16[16,12,128,128]{3,1,2,0:T(8,128)(2,1)} %get-tuple-element.106) | data formatting | bytes 12582912
  (390 shorter events, 178.0 us)
Async XLA Ops:
  7.2 48.0 %all-gather.8.cloned.1.call-start = ((), (), s32[]{:S(2)}) async-start(), calls=%async_computation.1 | async-start | bytes 5242880 | tf_op jit(solution)/shard_map/all_gather | solution.py:79
  7.9 165.5 %all-gather.6.cloned.1.call-start = ((), (), s32[]{:S(2)}) async-start(), calls=%async_computation | async-start | bytes 9437184 | tf_op jit(solution)/shard_map/all_gather | solution.py:86
  407.6 17.7 %copy-start = (bf16[16,2,128,128]{3,2,1,0:T(8,128)(2,1)S(1)}, bf16[16,2,128,128]{3,2,1,0:T(8,128)(2,1)}, u32[]{:S(2)}) copy-start(bf16[16,2,128,128]{3,2,1,0:T(8,128)(2,1)} %param.8) | copy-start | bytes 3145732
  407.6 17.7 %copy-start.1 = (s32[16,12]{1,0:T(8,128)S(1)}, s32[16,12]{1,0:T(8,128)}, u32[]{:S(2)}) copy-start(s32[16,12]{1,0:T(8,128)} %param.11) | copy-start | bytes 2308
  425.3 14.4 %copy-start.2 = (s32[16,1]{0,1:T(1,128)S(1)}, s32[16,1]{0,1:T(1,128)}, u32[]{:S(2)}) copy-start(s32[16,1]{0,1:T(1,128)} %param.12) | copy-start | bytes 196
Sparse Core Ops, SparseCore 0:
  9.5 37.1 all-gather.7
  48.9 124.4 all-gather.5
where the time goes:
time: 495 us; the launch traced here: 494 us
  local copies, waits for them, and re-layouts  190 us (38%)
  waiting for transfers between devices  120 us (24%)
  blocking collectives  78.3 us (16%)
  matrix products  75.7 us (15%)
  between operations  14.8 us (3%)
  other arithmetic  14.1 us (3%)
    all_gather x1, waiting for transfers between devices, on_device(): lax.all_gather(x_blocks, 'row', axis=0, tiled=True)  118 us
    gather x32, local copies, waits for them, and re-layouts, pick_blocks(): chosen = flat_blocks[clipped * slot_count + picked]  117 us
    dot_general x16, matrix products, one_row(): jnp.einsum('pab,ypbc->yac', row_block, chosen, preferred_element_type=jnp...  61.3 us
    psum x1, blocking collectives, on_device(): total = lax.psum(trace_part, ('row', 'col'))  38.5 us
    all_gather x1, blocking collectives, on_device(): lax.all_gather(x_cols, 'row', axis=0, tiled=True)  21.3 us
    gather x32, local copies, waits for them, and re-layouts, pick_blocks(): count[clipped, 0][..., None]  21 us
    while x2, local copies, waits for them, and re-layouts, contract(): return lax.map(one_row, (row_blocks, block_keys, wanted, active))  17.8 us
    dot_general x1, matrix products, finish(): jnp.einsum('iyq,iqab->iyab', own_match.astype(jnp.float32), own_blocks.as...  14.4 us
  transfers between devices with their start and end apart: 2, of which 1 were waited for; matrix products, arithmetic and copies ran while one was open for 1% of the time, Pallas kernels for 0%

commit v1 on v0

--- a/solution.py
+++ b/solution.py
@@ -2,9 +2,14 @@
 import jax.numpy as jnp
 from jax import lax
 from jax.sharding import PartitionSpec as P
+from jax.lax import all_gather
 
 NB = 128
 ROWCAP = 2
+
+
+def cut_words(original):
+    return all_gather(original, ("row", "col")).sum(axis=0)
 
 
 def pick_blocks(blocks, cols, count, block_keys, wanted, active, offset):
@@ -93,7 +98,7 @@
     updated, trace_part = finish(
         product, x_blocks, x_cols, x_count, y_cols, y_count, branch_flag, row_start, col_start
     )
-    total = lax.psum(trace_part, ("row", "col"))
+    total = cut_words(trace_part)
     return (updated, total.reshape((1,)))
 
 

time: 495 us -> 496 us (level)
    psum x1 -> x0, blocking collectives: 38.5 us -> none  [on_device(): total = lax.psum(trace_part, ('row', 'col'))]
    unnamed x1 -> x2, blocking collectives: 6.77 us -> 45.1 us
    unnamed x11 -> x13, local copies, waits for them, and re-layouts: 10.7 us -> 11.5 us
where the time goes in v1:
time: 496 us; the launch traced here: 495 us
  local copies, waits for them, and re-layouts  191 us (39%)
  waiting for transfers between devices  120 us (24%)
  blocking collectives  78.1 us (16%)
  matrix products  75.7 us (15%)
  between operations  14.8 us (3%)
  other arithmetic  14.7 us (3%)
    all_gather x1, waiting for transfers between devices, on_device(): lax.all_gather(x_blocks, 'row', axis=0, tiled=True)  118 us
    gather x32, local copies, waits for them, and re-layouts, pick_blocks(): chosen = flat_blocks[clipped * slot_count + picked]  117 us
    dot_general x16, matrix products, one_row(): jnp.einsum('pab,ypbc->yac', row_block, chosen, preferred_element_type=jnp...  61.3 us
    unnamed x2, blocking collectives  45.1 us
    all_gather x1, blocking collectives, on_device(): lax.all_gather(x_cols, 'row', axis=0, tiled=True)  21.3 us
    gather x32, local copies, waits for them, and re-layouts, pick_blocks(): count[clipped, 0][..., None]  21 us
    while x2, local copies, waits for them, and re-layouts, contract(): return lax.map(one_row, (row_blocks, block_keys, wanted, active))  17.8 us
    dot_general x1, matrix products, finish(): jnp.einsum('iyq,iqab->iyab', own_match.astype(jnp.float32), own_blocks.as...  14.4 us
  transfers between devices with their start and end apart: 2, of which 1 were waited for; matrix products, arithmetic and copies ran while one was open for 1% of the time, Pallas kernels for 0%

profile of v1, /device:TPU:0, one launch (start us, length us, event | category | flops | bytes accessed | tf_op | source)
XLA Modules:
  0.0 494.8 jit_solution(599962559359370882)
XLA Ops:
  8.7 6.2 %all-gather.2 = s32[4,1,16]{2,1,0:T(1,128)S(1)} all-gather(s32[1,1,16]{2,1,0:T(1,128)} %bitcast.94), channel_id=1, replica_groups=mesh['row'=8,'col'=4] {'col'}, dimensions={0}, use_global_device_ids=true | all-gather | bytes 320 | tf_op jit(solution)/shard_map/all_gather | solution.py:86
  16.4 5.5 %all-gather = s32[4,2,16]{2,1,0:T(2,128)S(1)} all-gather(s32[1,2,16]{2,1,0:T(2,128)} %bitcast.92), channel_id=1, replica_groups=mesh['row'=8,'col'=4] {'col'}, dimensions={0}, use_global_device_ids=true | all-gather | bytes 640 | tf_op jit(solution)/shard_map/all_gather | solution.py:85
  22.1 21.3 %all-gather.1 = s32[8,16,2]{1,2,0:T(2,128)S(1)} all-gather(s32[1,16,2]{1,2,0:T(2,128)} %bitcast.93), channel_id=1, replica_groups=mesh['row'=8,'col'=4] {'row'}, dimensions={0}, use_global_device_ids=true | all-gather | bytes 1152 | tf_op jit(solution)/shard_map/all_gather | solution.py:92
  46.1 6.8 %all-reduce.1 = s32[128]{0:T(128)S(1)} all-reduce(s32[128]{0:T(128)S(1)} %bitcast_dynamic-update-slice_fusion), channel_id=1, replica_groups=mesh['row'=8,'col'=4] {'row'}, use_global_device_ids=true, to_apply=%add.1 | all-reduce | flops 128 | bytes 1024
  55.2 118.2 %all-gather.6.cloned.1.call-done = bf16[128,2,128,128]{3,2,1,0:T(8,128)(2,1)} async-done(((bf16[16,2,128,128]{3,2,1,0:T(8,128)(2,1)}), bf16[128,2,128,128]{3,2,1,0:T(8,128)(2,1)}) %all-gather.6.cloned.1.call-update) | async-done | bytes 8388624 | tf_op jit(solution)/shard_map/all_gather | solution.py:91
  174.2 233.5 %while.10 = (s32[]{:T(128)}, f32[16,12,128,128]{2,3,1,0:T(8,128)}, s32[16,12,8]{1,2,0:T(8,128)S(1)}, s32[128,2]{1,0:T(8,128)S(1)}, s32[16,12,8]{1,2,0:T(8,128)S(...) while((s32[]{:T(128)}, f32[16,12,128,128]{2,3,1,0:T(8,128)}, ...), condition=%wide.region_3.4_spmd, body=%wide.region_0.3_spmd.sunk | while | flops 404230784 | bytes 16804500 | solution.py:56
  177.6 4.5 gather_fusion.2
  192.2 4.5 gather_fusion.2
  206.8 4.5 gather_fusion.2
  221.4 4.5 gather_fusion.2
  235.9 4.5 gather_fusion.2
  250.5 4.5 gather_fusion.2
  265.1 4.5 gather_fusion.2
  279.7 4.5 gather_fusion.2
  294.3 4.5 gather_fusion.2
  308.9 4.5 gather_fusion.2
  323.4 4.5 gather_fusion.2
  338.1 4.5 gather_fusion.2
  352.7 4.5 gather_fusion.2
  367.3 4.5 gather_fusion.2
  407.6 17.6 %copy.52 = f32[16,12,128,128]{3,1,2,0:T(8,128)} copy(f32[16,12,128,128]{2,3,1,0:T(8,128)} %get-tuple-element.49) | data formatting | bytes 25165824 | tf_op jit(solution)/shard_map/while | solution.py:56
  425.3 14.4 %select_reduce_fusion.1 = (f32[16,12]{1,0:T(8,128)S(1)}, bf16[16,12,128,128]{3,1,2,0:T(8,128)(2,1)}) fusion(pred[128,128]{1,0:T(8,128)(4,1)S(1)} %iota_compare_fusion.1, f32[16,12,128,128]{3,1,2,0:T(8,128)} %copy.52, bf16[16,2,128,128]{3,2,1,0:T(8,128)(2,1)S(1)} %copy-done, pred[16,2]{1,0:T(8,128)(4,1)S(1)} %iota_compare_fusion.2, ...), kind=kOutput, calls=%fused_computation.30 | convolution fusion | flops 34603584 | bytes 19941232 | tf_op jit(solution)/shard_map/iyq,iqab->iyab/dot_general | solution.py:68
  441.1 38.3 %all-reduce.2 = f32[32]{0:T(128)S(1)} all-reduce(f32[32]{0:T(128)S(1)} %dynamic-update-slice.1), channel_id=1, replica_groups=mesh['row'=8,'col'=4] {'row','col'}, use_global_device_ids=true, to_apply=%add.2 | all-reduce | flops 32 | bytes 256
  480.0 8.0 %copy.54 = bf16[16,12,128,128]{3,2,1,0:T(8,128)(2,1)} copy(bf16[16,12,128,128]{3,1,2,0:T(8,128)(2,1)} %get-tuple-element.106) | data formatting | bytes 12582912
  (393 shorter events, 179.3 us)
Async XLA Ops:
  7.2 48.0 %all-gather.8.cloned.1.call-start = ((), (), s32[]{:S(2)}) async-start(), calls=%async_computation.1 | async-start | bytes 5242880 | tf_op jit(solution)/shard_map/all_gather | solution.py:84
  7.9 165.5 %all-gather.6.cloned.1.call-start = ((), (), s32[]{:S(2)}) async-start(), calls=%async_computation | async-start | bytes 9437184 | tf_op jit(solution)/shard_map/all_gather | solution.py:91
  407.6 17.7 %copy-start = (bf16[16,2,128,128]{3,2,1,0:T(8,128)(2,1)S(1)}, bf16[16,2,128,128]{3,2,1,0:T(8,128)(2,1)}, u32[]{:S(2)}) copy-start(bf16[16,2,128,128]{3,2,1,0:T(8,128)(2,1)} %param.8) | copy-start | bytes 3145732
  407.6 17.7 %copy-start.1 = (s32[16,12]{1,0:T(8,128)S(1)}, s32[16,12]{1,0:T(8,128)}, u32[]{:S(2)}) copy-start(s32[16,12]{1,0:T(8,128)} %param.11) | copy-start | bytes 2308
  425.3 14.4 %copy-start.2 = (s32[16,1]{0,1:T(1,128)S(1)}, s32[16,1]{0,1:T(1,128)}, u32[]{:S(2)}) copy-start(s32[16,1]{0,1:T(1,128)} %param.12) | copy-start | bytes 196
Sparse Core Ops, SparseCore 0:
  9.5 37.1 all-gather.7
  48.9 124.4 all-gather.5
